TPU v7x, 32 devices: a whole 2x2x4 slice. The times are simulated.
32 devices in a mesh: gz: 2 (over x), gy: 4 (over y, core), gx: 4 (over z).
Axes of the slice: x: 2, y: 2, z: 4, core: 2. Of those that a mesh axis runs over, the one named last changes fastest.
Arguments:
- density: float32 [32, 64, 256], P('gx', 'gy', 'gz'), may hold values from 0.05 to 0.95
- spread: float32 [32, 64, 256], P('gx', 'gy', 'gz'), may hold values from 0.05 to 0.3
- sensitivities: float32 [9, 32, 64, 256], P(None, 'gx', 'gy', 'gz'), may hold values from -180 to 180, as said below
- violation: float32 [9], replicated, may hold values from -0.05 to 0.15
- multipliers_start: float32 [9], replicated, may hold values from 0.1 to 10
Outputs:
- new_density: float32 [32, 64, 256], P('gx', 'gy', 'gz')
- multipliers: float32 [9], replicated
Inputs may be any that keep to these rules, and one draw needn't show every extreme that they name: `sensitivities`: Real-valued, independent from voxel to voxel.
All inputs are finite; a program needn't handle non-finite values.
Results may differ from a plain program's by a relative error of at most 0.0003.
Values sent between devices are 32-bit elements; how exact they have to be, the bound alone decides.
A program may use at most 64 MiB of HBM per device.

v0:
```python
import math
import jax
import jax.numpy as jnp
from jax import lax
from jax.sharding import PartitionSpec as P

FIELDS = 9
ITERS = 3
RADIUS = 3.0
RAA = 1e-05
MOVE = 0.9
REG = 0.001
FLOOR = 0.2


def padded_2(block, sides, width):
    for axis, dim in sides:
        count = lax.axis_size(axis)
        forward = [(i, i + 1) for i in range(count - 1)]
        backward = [(target, source) for source, target in forward]
        low = lax.ppermute(
            lax.slice_in_dim(block, block.shape[dim] - width, None, axis=dim), axis, forward
        )
        high = lax.ppermute(lax.slice_in_dim(block, 0, width, axis=dim), axis, backward)
        block = jnp.concatenate([low, block, high], axis=dim)
    return block


def smooth(padded, nx, ny, nz):
    total = None
    for a in (-1, 0, 1):
        for b in (-1, 0, 1):
            for c in (-1, 0, 1):
                weight = RADIUS - math.sqrt(a * a + b * b + c * c)
                piece = padded[..., 1 + a : 1 + a + nx, 1 + b : 1 + b + ny, 1 + c : 1 + c + nz]
                total = weight * piece if total is None else total + weight * piece
    return total


def inside(index, extent, count):
    first = (index > 0).astype(jnp.float32)
    last = (index < extent - 1).astype(jnp.float32)
    return jnp.concatenate([first[None], jnp.ones((count,), jnp.float32), last[None]])


def totals(gradient_part, schur_part):
    return lax.psum((gradient_part, schur_part), ("gz", "gy", "gx"))


def shards(density, spread, sensitivities, violation, multipliers_start):
    nx, ny, nz = density.shape
    padded = padded_2(sensitivities, (("gz", 3), ("gy", 2), ("gx", 1)), 1)
    mask_x = inside(lax.axis_index("gx"), lax.axis_size("gx"), nx)
    mask_y = inside(lax.axis_index("gy"), lax.axis_size("gy"), ny)
    mask_z = inside(lax.axis_index("gz"), lax.axis_size("gz"), nz)
    valid = mask_x[:, None, None] * mask_y[None, :, None] * mask_z[None, None, :]
    denom = smooth(valid, nx, ny, nz)
    filtered = smooth(padded, nx, ny, nz) / denom[None]
    cells = nx * ny * nz
    dens = density.reshape(-1)
    span = spread.reshape(-1)
    rows = jnp.concatenate(
        [filtered.reshape(FIELDS, cells), jnp.ones((1, cells), jnp.float32)], axis=0
    )
    grow = jnp.maximum(rows, 0.0)
    fall = jnp.maximum(-rows, 0.0)
    square = span * span
    pp = square * (1.001 * grow + 0.001 * fall + RAA)
    qq = square * (0.001 * grow + 1.001 * fall + RAA)
    lower = dens - span
    upper = dens + span
    floor_x = jnp.maximum(0.0, dens - MOVE * span)
    ceil_x = jnp.minimum(1.0, dens + MOVE * span)
    base = (pp[1:] + qq[1:]) / span
    keep = 1.0 - violation
    base_local = jnp.sum(base, axis=1)
    bound = None
    bound = keep * lax.psum(base_local, ("gz", "gy", "gx"))

    def respond(lam):
        weights = jnp.concatenate([jnp.ones((1,), jnp.float32), lam])
        big_p = jnp.dot(weights, pp, precision=lax.Precision.HIGHEST)
        big_q = jnp.dot(weights, qq, precision=lax.Precision.HIGHEST)
        root_p = jnp.sqrt(big_p)
        root_q = jnp.sqrt(big_q)
        moved = (root_p * lower + root_q * upper) / (root_p + root_q)
        return (jnp.clip(moved, floor_x, ceil_x), big_p, big_q)

    lam = multipliers_start
    for step in range(ITERS):
        moved, big_p, big_q = respond(lam)
        above = upper - moved
        below = moved - lower
        values = pp[1:] / above + qq[1:] / below
        slopes = pp[1:] / (above * above) - qq[1:] / (below * below)
        curv = 2.0 * big_p / (above * above * above) + 2.0 * big_q / (below * below * below)
        schur_part = jnp.dot(slopes / curv, slopes.T, precision=lax.Precision.HIGHEST)
        summed, schur = totals(jnp.sum(values, axis=1), schur_part)
        gradient = summed - bound
        shift = REG * jnp.trace(schur) / FIELDS
        system = schur + shift * jnp.eye(FIELDS, dtype=jnp.float32)
        factor = jnp.linalg.cholesky(system)
        delta = jax.scipy.linalg.cho_solve((factor, True), gradient)
        lam = jnp.maximum(lam + delta, FLOOR * lam)
    moved, big_p, big_q = respond(lam)
    return (moved.reshape(nx, ny, nz), lam)


def solution(mesh):
    return jax.shard_map(
        shards,
        mesh=mesh,
        in_specs=(P("gx", "gy", "gz"), P("gx", "gy", "gz"), P(None, "gx", "gy", "gz"), P(), P()),
        out_specs=(P("gx", "gy", "gz"), P()),
        check_vma=False,
    )
```

profile of v0, /device:TPU:0, one launch (start us, length us, event | category | flops | bytes accessed | tf_op | source)
XLA Modules:
  0.0 187.6 jit_solution(5219307162577140861)
XLA Ops:
  0.6 1.5 fusion.136
  2.2 0.5 copy.82
  2.7 4.9 %collective-permute-start = (f32[9,8,16,1]{2,1,3,0:T(8,128)S(1)}, f32[9,8,16,1]{2,1,3,0:T(8,128)S(1)}, u32[]{:S(2)}, u32[]{:S(2)}) collective-permute-start(f32[9,8,16,1]{2,1,3,0:T(8,128)S(1)} %copy.82), channel_id=1, source_target_pairs={{0,16},{1,17},{2,18},{3,19},{4,20},{5,21},{6,22},{7,23},{8,24},{9,... | collective-permute-start | bytes 13832 | tf_op jit(solution)/shard_map/ppermute | solution.py:21
  7.5 0.5 copy.83
  8.0 1.3 collective-permute-start.1
  9.8 0.2 copy.58
  10.0 0.5 copy.57
  10.5 3.4 %collective-permute-done.1 = f32[9,8,16,1]{2,1,3,0:T(8,128)S(1)} collective-permute-done((f32[9,8,16,1]{2,1,3,0:T(8,128)S(1)}, f32[9,8,16,1]{2,1,3,0:T(8,128)S(1)}, u32[]{:S(2)}, u32[]{:S(2)}) %collective-permute-start.1) | collective-permute-done | bytes 4640 | tf_op jit(solution)/shard_map/ppermute | solution.py:24
  13.9 0.5 copy.59
  14.5 1.3 collective-permute-start.2
  15.8 1.3 collective-permute-start.3
  17.1 0.4 fusion.66
  17.5 3.2 %collective-permute-done.3 = f32[9,8,1,130]{3,1,2,0:T(8,128)S(1)} collective-permute-done((f32[9,8,1,130]{3,1,2,0:T(8,128)S(1)}, f32[9,8,1,130]{3,1,2,0:T(8,128)S(1)}, u32[]{:S(2)}, u32[]{:S(2)}) %collective-permute-start.3) | collective-permute-done | bytes 37472 | tf_op jit(solution)/shard_map/ppermute | solution.py:24
  20.7 1.0 pad_maximum_fusion.8
  21.7 3.5 %collective-permute-start.4 = (f32[9,1,18,130]{3,2,1,0:T(8,128)S(1)}, f32[9,1,18,130]{3,2,1,0:T(8,128)S(1)}, u32[]{:S(2)}, u32[]{:S(2)}) collective-permute-start(f32[9,1,18,130]{3,2,1,0:T(8,128)S(1)} %copy.60), channel_id=1, source_target_pairs={{0,1},{1,2},{2,3},{4,5},{5,6},{6,7},{8,9},{9,10},{10,11},{12,13},{... | collective-permute-start | bytes 252728 | tf_op jit(solution)/shard_map/ppermute | solution.py:21
  25.3 1.5 collective-permute-start.5
  26.7 1.0 maximum_maximum_fusion.1
  27.7 1.3 collective-permute-done.4
  29.0 0.2 copy.61
  29.2 4.5 %collective-permute-done.5 = f32[9,1,18,130]{3,2,1,0:T(8,128)S(1)} collective-permute-done((f32[9,1,18,130]{3,2,1,0:T(8,128)S(1)}, f32[9,1,18,130]{3,2,1,0:T(8,128)S(1)}, u32[]{:S(2)}, u32[]{:S(2)}) %collective-permute-start.5) | collective-permute-done | bytes 84272 | tf_op jit(solution)/shard_map/ppermute | solution.py:24
  33.7 0.2 copy.68
  33.9 2.1 %maximum_maximum_fusion = (f32[9,9,18,130]{3,1,2,0:T(8,128)S(1)}, f32[9,9,18,130]{3,1,2,0:T(8,128)S(1)}) fusion(f32[9,8,1,130]{3,1,2,0:T(8,128)S(1)} %collective-permute-done.3, f32[9,8,16,1]{3,1,2,0:T(8,128)S(1)} %copy.59, f32[9,8,16,128]{3,1,2,0:T(8,128)S(1)} %copy.58, f32[9,8,16,1]{3,1,2,0:T(8,128)S(1)} %copy.57, ...), kind=kLoop, calls=%fused_computation | loop fusion | flops 1895400 | bytes 2358720 | tf_op jit(solution)/shard_map/concatenate | solution.py:25
  36.0 3.1 %fusion.29 = f32[9,8,16,128]{3,1,2,0:T(8,128)S(1)} fusion(f32[9,9,18,130]{3,1,2,0:T(8,128)S(1)} %get-tuple-element.33, f32[9,8,17,130]{3,1,2,0:T(8,128)S(1)} %get-tuple-element.37, f32[9,8,16,1]{3,1,2,0:T(8,128)S(1)} %copy.59, f32[9,8,16,128]{3,1,2,0:T(8,128)S(1)} %copy.58, f32[9,8,16,1]{3,1,2,0:T(8,128)S(1)} %copy.57, ...), kind=kLoop, calls=%fused_computation.47 | loop fusion | flops 8257536 | bytes 15410176 | tf_op jit(solution)/shard_map/div | solution.py:58
  39.4 0.6 copy.84
  40.0 0.5 add_multiply_fusion.1
  40.5 0.6 fusion.122
  41.2 0.6 fusion.124
  41.9 0.8 fusion.21
  42.8 1.7 fusion.4
  44.5 40.1 %all-reduce.3 = (f32[9,9]{0,1:T(8,128)S(1)}, f32[9]{0:T(128)S(1)}, f32[9]{0:T(128)S(1)}) all-reduce(f32[9,9]{0,1:T(8,128)S(1)} %fusion.4, f32[9]{0:T(128)S(1)} %get-tuple-element.5, f32[9]{0:T(128)S(1)} %get-tuple-element.4), channel_id=1, replica_groups=mesh['gz'=2,'gy'=4,'gx'=4] {'gz','gy','gx'}, use_global_device_ids=true, to_apply=%region_0.0 | all-reduce | flops 99 | bytes 792 | tf_op jit(solution)/shard_map/psum | solution.py:47
  84.6 0.6 select_reduce_fusion.5
  86.0 0.8 cholesky.59
  86.8 0.6 compare_reduce_fusion.2
  87.5 0.6 fusion.92
  88.1 0.7 custom-call.9
  88.8 0.1 convolution_bitcast_fusion.5
  89.0 0.1 fusion.9
  89.1 0.7 fusion.120
  89.8 0.6 fusion.118
  90.5 0.5 add_reduce_fusion.1
  91.0 1.7 fusion.2
  92.7 40.2 %all-reduce.2 = (f32[9,9]{0,1:T(8,128)S(1)}, f32[9]{0:T(128)S(1)}) all-reduce(f32[9,9]{0,1:T(8,128)S(1)} %fusion.2, f32[9]{0:T(128)S(1)} %add_reduce_fusion.1), channel_id=1, replica_groups=mesh['gz'=2,'gy'=4,'gx'=4] {'gz','gy','gx'}, use_global_device_ids=true, to_apply=%region_8.11 | all-reduce | flops 90 | bytes 720 | tf_op jit(solution)/shard_map/psum | solution.py:47
  132.9 0.6 select_reduce_fusion.4
  134.2 0.8 cholesky.70
  135.1 0.6 compare_reduce_fusion.1
  135.7 0.6 fusion.93
  136.4 0.7 custom-call.10
  137.1 0.1 convolution_bitcast_fusion.3
  137.2 0.1 fusion.10
  137.4 0.7 fusion.116
  138.0 0.6 fusion.114
  138.8 0.5 add_reduce_fusion
  139.3 1.7 fusion
  140.9 40.1 %all-reduce.1 = (f32[9,9]{0,1:T(8,128)S(1)}, f32[9]{0:T(128)S(1)}) all-reduce(f32[9,9]{0,1:T(8,128)S(1)} %fusion, f32[9]{0:T(128)S(1)} %add_reduce_fusion), channel_id=1, replica_groups=mesh['gz'=2,'gy'=4,'gx'=4] {'gz','gy','gx'}, use_global_device_ids=true, to_apply=%region_12.15 | all-reduce | flops 90 | bytes 720 | tf_op jit(solution)/shard_map/psum | solution.py:47
  181.1 0.6 select_reduce_fusion.3
  182.4 0.8 cholesky.81
  183.3 0.6 compare_reduce_fusion
  183.9 0.6 fusion.94
  184.6 0.7 custom-call.11
  185.3 0.1 convolution_bitcast_fusion.1
  185.4 0.1 fusion.11
  185.6 0.7 fusion.128
  186.2 0.6 fusion.126
  186.9 0.7 maximum_minimum_fusion
  (49 shorter events, 1.7 us)
Async XLA Ops:
  0.6 9.2 %copy-start = (f32[9,8,16,128]{3,2,1,0:T(8,128)S(1)}, f32[9,8,16,128]{3,2,1,0:T(8,128)}, u32[]{:S(2)}) copy-start(f32[9,8,16,128]{3,2,1,0:T(8,128)} %param.10) | copy-start | bytes 1769476
  2.7 7.4 %collective-permute-start = (f32[9,8,16,1]{2,1,3,0:T(8,128)S(1)}, f32[9,8,16,1]{2,1,3,0:T(8,128)S(1)}, u32[]{:S(2)}, u32[]{:S(2)}) collective-permute-start(f32[9,8,16,1]{2,1,3,0:T(8,128)S(1)} %copy.82), channel_id=1, source_target_pairs={{0,16},{1,17},{2,18},{3,19},{4,20},{5,21},{6,22},{7,23},{8,24},{9,... | collective-permute-start | bytes 13832 | tf_op jit(solution)/shard_map/ppermute | solution.py:21
  8.0 5.9 %collective-permute-start.1 = (f32[9,8,16,1]{2,1,3,0:T(8,128)S(1)}, f32[9,8,16,1]{2,1,3,0:T(8,128)S(1)}, u32[]{:S(2)}, u32[]{:S(2)}) collective-permute-start(f32[9,8,16,1]{2,1,3,0:T(8,128)S(1)} %copy.83), channel_id=1, source_target_pairs={{16,0},{17,1},{18,2},{19,3},{20,4},{21,5},{22,6},{23,7},{24,8},{25... | collective-permute-start | bytes 13832 | tf_op jit(solution)/shard_map/ppermute | solution.py:24
  10.0 7.5 %copy-start.1 = (f32[8,16,128]{2,1,0:T(8,128)S(1)}, f32[8,16,128]{2,1,0:T(8,128)}, u32[]{:S(2)}) copy-start(f32[8,16,128]{2,1,0:T(8,128)} %param.9) | copy-start | bytes 196612
  14.5 3.0 %collective-permute-start.2 = (f32[9,8,1,130]{3,1,2,0:T(8,128)S(1)}, f32[9,8,1,130]{3,1,2,0:T(8,128)S(1)}, u32[]{:S(2)}, u32[]{:S(2)}) collective-permute-start(f32[9,8,1,130]{3,1,2,0:T(8,128)S(1)} %get-tuple-element.38), channel_id=1, source_target_pairs={{0,4},{4,8},{8,12},{1,5},{5,9},{9,13},{2,6},{6,10},{10,14},{3,7},{... | collective-permute-start | bytes 112328 | tf_op jit(solution)/shard_map/ppermute | solution.py:21
  15.8 4.9 %collective-permute-start.3 = (f32[9,8,1,130]{3,1,2,0:T(8,128)S(1)}, f32[9,8,1,130]{3,1,2,0:T(8,128)S(1)}, u32[]{:S(2)}, u32[]{:S(2)}) collective-permute-start(f32[9,8,1,130]{3,1,2,0:T(8,128)S(1)} %get-tuple-element.39), channel_id=1, source_target_pairs={{4,0},{8,4},{12,8},{5,1},{9,5},{13,9},{6,2},{10,6},{14,10},{7,3},{... | collective-permute-start | bytes 112328 | tf_op jit(solution)/shard_map/ppermute | solution.py:24
  21.7 7.3 %collective-permute-start.4 = (f32[9,1,18,130]{3,2,1,0:T(8,128)S(1)}, f32[9,1,18,130]{3,2,1,0:T(8,128)S(1)}, u32[]{:S(2)}, u32[]{:S(2)}) collective-permute-start(f32[9,1,18,130]{3,2,1,0:T(8,128)S(1)} %copy.60), channel_id=1, source_target_pairs={{0,1},{1,2},{2,3},{4,5},{5,6},{6,7},{8,9},{9,10},{10,11},{12,13},{... | collective-permute-start | bytes 252728 | tf_op jit(solution)/shard_map/ppermute | solution.py:21
  25.3 8.4 %collective-permute-start.5 = (f32[9,1,18,130]{3,2,1,0:T(8,128)S(1)}, f32[9,1,18,130]{3,2,1,0:T(8,128)S(1)}, u32[]{:S(2)}, u32[]{:S(2)}) collective-permute-start(f32[9,1,18,130]{3,2,1,0:T(8,128)S(1)} %copy.67), channel_id=1, source_target_pairs={{1,0},{2,1},{3,2},{5,4},{6,5},{7,6},{9,8},{10,9},{11,10},{13,12},{... | collective-permute-start | bytes 252728 | tf_op jit(solution)/shard_map/ppermute | solution.py:24
  39.3 1.2 copy-start.3
  40.0 1.8 copy-start.2
  42.8 46.0 %copy-start.5 = (f32[9]{0:T(128)S(1)}, f32[9]{0:T(128)}, u32[]{:S(2)}) copy-start(f32[9]{0:T(128)} %param.11) | copy-start | bytes 112
  185.6 2.0 %copy-start.4 = (f32[9]{0:T(128)}, f32[9]{0:T(128)S(1)}, u32[]{:S(2)}) copy-start(f32[9]{0:T(128)S(1)} %fusion.11) | copy-start | bytes 112
where the time goes:
time: 188 us
  blocking collectives  120 us (64%)
  other arithmetic  21.8 us (12%)
  starting transfers between devices  13.7 us (7%)
  waiting for transfers between devices  12.4 us (7%)
  matrix products  11 us (6%)
  local copies, waits for them, and re-layouts  5.18 us (3%)
  between operations  3.06 us (2%)
    psum x3, blocking collectives, totals(): return lax.psum((gradient_part, schur_part), ('gz', 'gy', 'gx'))  120 us
    ppermute x3, waiting for transfers between devices, padded_2(): lax.ppermute(lax.slice_in_dim(block, 0, width, axis=dim), axis, backward)  11.1 us
    ppermute x3, starting transfers between devices, padded_2(): lax.ppermute(lax.slice_in_dim(block, block.shape[dim] - width, None, axis...  9.67 us
    dot_general x3, matrix products, shards(): jnp.dot(slopes / curv, slopes.T, precision=lax.Precision.HIGHEST)  5.02 us
    another operation x9, other arithmetic, shards(): factor = jnp.linalg.cholesky(system)  4.45 us
    ppermute x3, starting transfers between devices, padded_2(): lax.ppermute(lax.slice_in_dim(block, 0, width, axis=dim), axis, backward)  4.06 us
    another operation x6, other arithmetic, shards(): delta = jax.scipy.linalg.cho_solve((factor, True), gradient)  4.03 us
  transfers between devices with their start and end apart: 6, of which 4 were waited for; matrix products, arithmetic and copies ran while one was open for 2% of the time, Pallas kernels for 0%

commit v1 on v0

--- a/solution.py
+++ b/solution.py
@@ -3,6 +3,7 @@
 import jax.numpy as jnp
 from jax import lax
 from jax.sharding import PartitionSpec as P
+from jax.lax import psum
 
 FIELDS = 9
 ITERS = 3
@@ -44,7 +45,7 @@
 
 
 def totals(gradient_part, schur_part):
-    return lax.psum((gradient_part, schur_part), ("gz", "gy", "gx"))
+    return psum(psum((gradient_part, schur_part), axis_name=("gy", "gx")), axis_name="gz")
 
 
 def shards(density, spread, sensitivities, violation, multipliers_start):

time: 188 us -> 219 us (1.16)
  blocking collectives: 120 us -> 152 us
    psum x3 -> x7, blocking collectives: 120 us -> 152 us  [the longest x3 97.5 us: totals(): psum((gradient_part, schur_part), axis_name=('gy', 'gx'))]
  transfers between devices with their start and end apart: 6 -> 6, of which waited for: 4 -> 4; matrix products, arithmetic and copies ran while one was open for 2% -> 1% of each run, Pallas kernels for 0% -> 0%
where the time goes in v1:
time: 219 us
  blocking collectives  152 us (69%)
  other arithmetic  21.8 us (10%)
  starting transfers between devices  13.7 us (6%)
  waiting for transfers between devices  12.4 us (6%)
  matrix products  11 us (5%)
  local copies, waits for them, and re-layouts  5.18 us (2%)
  between operations  3.08 us (1%)
    psum x3, blocking collectives, totals(): psum((gradient_part, schur_part), axis_name=('gy', 'gx'))  97.5 us
    psum x1, blocking collectives, shards(): bound = keep * lax.psum(base_local, ('gz', 'gy', 'gx'))  38.9 us
    psum x3, blocking collectives, totals(): psum(psum((gradient_part, schur_part), axis_name=('gy', 'gx')), axis_name...  15.2 us
    ppermute x3, waiting for transfers between devices, padded_2(): lax.ppermute(lax.slice_in_dim(block, 0, width, axis=dim), axis, backward)  11.1 us
    ppermute x3, starting transfers between devices, padded_2(): lax.ppermute(lax.slice_in_dim(block, block.shape[dim] - width, None, axis...  9.67 us
    dot_general x3, matrix products, shards(): jnp.dot(slopes / curv, slopes.T, precision=lax.Precision.HIGHEST)  5.02 us
    another operation x9, other arithmetic, shards(): factor = jnp.linalg.cholesky(system)  4.45 us
  transfers between devices with their start and end apart: 6, of which 4 were waited for; matrix products, arithmetic and copies ran while one was open for 1% of the time, Pallas kernels for 0%

profile of v1, /device:TPU:0, one launch (start us, length us, event | category | flops | bytes accessed | tf_op | source)
XLA Modules:
  0.0 218.8 jit_solution(12521374528929716191)
XLA Ops:
  0.6 1.5 fusion.136
  2.2 0.5 copy.82
  2.7 4.9 %collective-permute-start = (f32[9,8,16,1]{2,1,3,0:T(8,128)S(1)}, f32[9,8,16,1]{2,1,3,0:T(8,128)S(1)}, u32[]{:S(2)}, u32[]{:S(2)}) collective-permute-start(f32[9,8,16,1]{2,1,3,0:T(8,128)S(1)} %copy.82), channel_id=1, source_target_pairs={{0,16},{1,17},{2,18},{3,19},{4,20},{5,21},{6,22},{7,23},{8,24},{9,... | collective-permute-start | bytes 13832 | tf_op jit(solution)/shard_map/ppermute | solution.py:22
  7.5 0.5 copy.83
  8.0 1.3 collective-permute-start.1
  9.8 0.2 copy.58
  10.0 0.5 copy.57
  10.5 3.4 %collective-permute-done.1 = f32[9,8,16,1]{2,1,3,0:T(8,128)S(1)} collective-permute-done((f32[9,8,16,1]{2,1,3,0:T(8,128)S(1)}, f32[9,8,16,1]{2,1,3,0:T(8,128)S(1)}, u32[]{:S(2)}, u32[]{:S(2)}) %collective-permute-start.1) | collective-permute-done | bytes 4640 | tf_op jit(solution)/shard_map/ppermute | solution.py:25
  13.9 0.5 copy.59
  14.5 1.3 collective-permute-start.2
  15.8 1.3 collective-permute-start.3
  17.1 0.4 fusion.66
  17.5 3.2 %collective-permute-done.3 = f32[9,8,1,130]{3,1,2,0:T(8,128)S(1)} collective-permute-done((f32[9,8,1,130]{3,1,2,0:T(8,128)S(1)}, f32[9,8,1,130]{3,1,2,0:T(8,128)S(1)}, u32[]{:S(2)}, u32[]{:S(2)}) %collective-permute-start.3) | collective-permute-done | bytes 37472 | tf_op jit(solution)/shard_map/ppermute | solution.py:25
  20.7 1.0 pad_maximum_fusion.8
  21.7 3.5 %collective-permute-start.4 = (f32[9,1,18,130]{3,2,1,0:T(8,128)S(1)}, f32[9,1,18,130]{3,2,1,0:T(8,128)S(1)}, u32[]{:S(2)}, u32[]{:S(2)}) collective-permute-start(f32[9,1,18,130]{3,2,1,0:T(8,128)S(1)} %copy.60), channel_id=1, source_target_pairs={{0,1},{1,2},{2,3},{4,5},{5,6},{6,7},{8,9},{9,10},{10,11},{12,13},{... | collective-permute-start | bytes 252728 | tf_op jit(solution)/shard_map/ppermute | solution.py:22
  25.3 1.5 collective-permute-start.5
  26.7 1.0 maximum_maximum_fusion.1
  27.7 1.3 collective-permute-done.4
  29.0 0.2 copy.61
  29.2 4.5 %collective-permute-done.5 = f32[9,1,18,130]{3,2,1,0:T(8,128)S(1)} collective-permute-done((f32[9,1,18,130]{3,2,1,0:T(8,128)S(1)}, f32[9,1,18,130]{3,2,1,0:T(8,128)S(1)}, u32[]{:S(2)}, u32[]{:S(2)}) %collective-permute-start.5) | collective-permute-done | bytes 84272 | tf_op jit(solution)/shard_map/ppermute | solution.py:25
  33.7 0.2 copy.68
  33.9 2.1 maximum_maximum_fusion
  36.0 3.1 %fusion.29 = f32[9,8,16,128]{3,1,2,0:T(8,128)S(1)} fusion(f32[9,9,18,130]{3,1,2,0:T(8,128)S(1)} %get-tuple-element.38, f32[9,8,17,130]{3,1,2,0:T(8,128)S(1)} %get-tuple-element.42, f32[9,8,16,1]{3,1,2,0:T(8,128)S(1)} %copy.59, f32[9,8,16,128]{3,1,2,0:T(8,128)S(1)} %copy.58, f32[9,8,16,1]{3,1,2,0:T(8,128)S(1)} %copy.57, ...), kind=kLoop, calls=%fused_computation.47 | loop fusion | flops 8257536 | bytes 15410176 | tf_op jit(solution)/shard_map/div | solution.py:59
  39.4 0.6 copy.84
  40.0 0.5 add_multiply_fusion.1
  40.5 0.6 fusion.122
  41.2 0.6 fusion.124
  41.9 0.8 fusion.21
  42.8 1.7 fusion.4
  44.5 32.7 %all-reduce.3 = (f32[9,9]{0,1:T(8,128)S(1)}, f32[9]{0:T(128)S(1)}) all-reduce(f32[9,9]{0,1:T(8,128)S(1)} %fusion.4, f32[9]{0:T(128)S(1)} %get-tuple-element.5), channel_id=1, replica_groups=mesh['gz'=2,'gy'=4,'gx'=4] {'gy','gx'}, use_global_device_ids=true, to_apply=%region_0.0 | all-reduce | flops 90 | bytes 720 | tf_op jit(solution)/shard_map/psum | solution.py:48
  77.2 5.1 %all-reduce.6 = (f32[9,9]{0,1:T(8,128)S(1)}, f32[9]{0:T(128)S(1)}) all-reduce(f32[9,9]{0,1:T(8,128)S(1)} %get-tuple-element.10, f32[9]{0:T(128)S(1)} %get-tuple-element.11), channel_id=1, replica_groups=mesh['gz'=2,'gy'=4,'gx'=4] {'gz'}, use_global_device_ids=true, to_apply=%region_1.0 | all-reduce | flops 90 | bytes 720 | tf_op jit(solution)/shard_map/psum | solution.py:48
  82.3 0.6 select_reduce_fusion.5
  83.7 0.8 cholesky.59
  84.5 0.6 compare_reduce_fusion.2
  85.2 0.6 fusion.92
  85.8 0.7 custom-call.9
  86.5 38.9 %psum.95 = f32[9]{0:T(128)S(1)} all-reduce(f32[9]{0:T(128)S(1)} %get-tuple-element.4), channel_id=1, replica_groups=mesh['gz'=2,'gy'=4,'gx'=4] {'gz','gy','gx'}, use_global_device_ids=true, to_apply=%region_9.11 | all-reduce | flops 9 | bytes 72 | tf_op jit(solution)/shard_map/psum | solution.py:79
  125.7 0.7 fusion.120
  126.4 0.6 fusion.118
  127.1 0.5 add_reduce_fusion.1
  127.6 1.7 fusion.2
  129.3 33.7 %all-reduce.2 = (f32[9,9]{0,1:T(8,128)S(1)}, f32[9]{0:T(128)S(1)}) all-reduce(f32[9,9]{0,1:T(8,128)S(1)} %fusion.2, f32[9]{0:T(128)S(1)} %add_reduce_fusion.1), channel_id=1, replica_groups=mesh['gz'=2,'gy'=4,'gx'=4] {'gy','gx'}, use_global_device_ids=true, to_apply=%region_10.13 | all-reduce | flops 90 | bytes 720 | tf_op jit(solution)/shard_map/psum | solution.py:48
  163.0 5.1 %all-reduce.5 = (f32[9,9]{0,1:T(8,128)S(1)}, f32[9]{0:T(128)S(1)}) all-reduce(f32[9,9]{0,1:T(8,128)S(1)} %get-tuple-element.8, f32[9]{0:T(128)S(1)} %get-tuple-element.9), channel_id=1, replica_groups=mesh['gz'=2,'gy'=4,'gx'=4] {'gz'}, use_global_device_ids=true, to_apply=%region_11.14 | all-reduce | flops 90 | bytes 720 | tf_op jit(solution)/shard_map/psum | solution.py:48
  168.1 0.6 select_reduce_fusion.4
  169.4 0.8 cholesky.70
  170.3 0.6 compare_reduce_fusion.1
  170.9 0.6 fusion.93
  171.6 0.7 custom-call.10
  172.3 0.1 convolution_bitcast_fusion.3
  172.6 0.7 fusion.116
  173.2 0.6 fusion.114
  174.0 0.5 add_reduce_fusion
  174.5 1.7 fusion
  176.1 31.1 %all-reduce.1 = (f32[9,9]{0,1:T(8,128)S(1)}, f32[9]{0:T(128)S(1)}) all-reduce(f32[9,9]{0,1:T(8,128)S(1)} %fusion, f32[9]{0:T(128)S(1)} %add_reduce_fusion), channel_id=1, replica_groups=mesh['gz'=2,'gy'=4,'gx'=4] {'gy','gx'}, use_global_device_ids=true, to_apply=%region_16.19 | all-reduce | flops 90 | bytes 720 | tf_op jit(solution)/shard_map/psum | solution.py:48
  207.2 5.1 %all-reduce.4 = (f32[9,9]{0,1:T(8,128)S(1)}, f32[9]{0:T(128)S(1)}) all-reduce(f32[9,9]{0,1:T(8,128)S(1)} %get-tuple-element.6, f32[9]{0:T(128)S(1)} %get-tuple-element.7), channel_id=1, replica_groups=mesh['gz'=2,'gy'=4,'gx'=4] {'gz'}, use_global_device_ids=true, to_apply=%region_17.20 | all-reduce | flops 90 | bytes 720 | tf_op jit(solution)/shard_map/psum | solution.py:48
  212.3 0.6 select_reduce_fusion.3
  213.7 0.8 cholesky.81
  214.5 0.6 compare_reduce_fusion
  215.2 0.6 fusion.94
  215.8 0.7 custom-call.11
  216.5 0.1 convolution_bitcast_fusion.1
  216.8 0.7 fusion.128
  217.5 0.6 fusion.126
  218.1 0.7 maximum_minimum_fusion
  (53 shorter events, 2.2 us)
Async XLA Ops:
  0.6 9.2 %copy-start = (f32[9,8,16,128]{3,2,1,0:T(8,128)S(1)}, f32[9,8,16,128]{3,2,1,0:T(8,128)}, u32[]{:S(2)}) copy-start(f32[9,8,16,128]{3,2,1,0:T(8,128)} %param.10) | copy-start | bytes 1769476
  2.7 7.4 %collective-permute-start = (f32[9,8,16,1]{2,1,3,0:T(8,128)S(1)}, f32[9,8,16,1]{2,1,3,0:T(8,128)S(1)}, u32[]{:S(2)}, u32[]{:S(2)}) collective-permute-start(f32[9,8,16,1]{2,1,3,0:T(8,128)S(1)} %copy.82), channel_id=1, source_target_pairs={{0,16},{1,17},{2,18},{3,19},{4,20},{5,21},{6,22},{7,23},{8,24},{9,... | collective-permute-start | bytes 13832 | tf_op jit(solution)/shard_map/ppermute | solution.py:22
  8.0 5.9 %collective-permute-start.1 = (f32[9,8,16,1]{2,1,3,0:T(8,128)S(1)}, f32[9,8,16,1]{2,1,3,0:T(8,128)S(1)}, u32[]{:S(2)}, u32[]{:S(2)}) collective-permute-start(f32[9,8,16,1]{2,1,3,0:T(8,128)S(1)} %copy.83), channel_id=1, source_target_pairs={{16,0},{17,1},{18,2},{19,3},{20,4},{21,5},{22,6},{23,7},{24,8},{25... | collective-permute-start | bytes 13832 | tf_op jit(solution)/shard_map/ppermute | solution.py:25
  10.0 7.5 %copy-start.1 = (f32[8,16,128]{2,1,0:T(8,128)S(1)}, f32[8,16,128]{2,1,0:T(8,128)}, u32[]{:S(2)}) copy-start(f32[8,16,128]{2,1,0:T(8,128)} %param.9) | copy-start | bytes 196612
  14.5 3.0 %collective-permute-start.2 = (f32[9,8,1,130]{3,1,2,0:T(8,128)S(1)}, f32[9,8,1,130]{3,1,2,0:T(8,128)S(1)}, u32[]{:S(2)}, u32[]{:S(2)}) collective-permute-start(f32[9,8,1,130]{3,1,2,0:T(8,128)S(1)} %get-tuple-element.43), channel_id=1, source_target_pairs={{0,4},{4,8},{8,12},{1,5},{5,9},{9,13},{2,6},{6,10},{10,14},{3,7},{... | collective-permute-start | bytes 112328 | tf_op jit(solution)/shard_map/ppermute | solution.py:22
  15.8 4.9 %collective-permute-start.3 = (f32[9,8,1,130]{3,1,2,0:T(8,128)S(1)}, f32[9,8,1,130]{3,1,2,0:T(8,128)S(1)}, u32[]{:S(2)}, u32[]{:S(2)}) collective-permute-start(f32[9,8,1,130]{3,1,2,0:T(8,128)S(1)} %get-tuple-element.44), channel_id=1, source_target_pairs={{4,0},{8,4},{12,8},{5,1},{9,5},{13,9},{6,2},{10,6},{14,10},{7,3},{... | collective-permute-start | bytes 112328 | tf_op jit(solution)/shard_map/ppermute | solution.py:25
  21.7 7.3 %collective-permute-start.4 = (f32[9,1,18,130]{3,2,1,0:T(8,128)S(1)}, f32[9,1,18,130]{3,2,1,0:T(8,128)S(1)}, u32[]{:S(2)}, u32[]{:S(2)}) collective-permute-start(f32[9,1,18,130]{3,2,1,0:T(8,128)S(1)} %copy.60), channel_id=1, source_target_pairs={{0,1},{1,2},{2,3},{4,5},{5,6},{6,7},{8,9},{9,10},{10,11},{12,13},{... | collective-permute-start | bytes 252728 | tf_op jit(solution)/shard_map/ppermute | solution.py:22
  25.3 8.4 %collective-permute-start.5 = (f32[9,1,18,130]{3,2,1,0:T(8,128)S(1)}, f32[9,1,18,130]{3,2,1,0:T(8,128)S(1)}, u32[]{:S(2)}, u32[]{:S(2)}) collective-permute-start(f32[9,1,18,130]{3,2,1,0:T(8,128)S(1)} %copy.67), channel_id=1, source_target_pairs={{1,0},{2,1},{3,2},{5,4},{6,5},{7,6},{9,8},{10,9},{11,10},{13,12},{... | collective-permute-start | bytes 252728 | tf_op jit(solution)/shard_map/ppermute | solution.py:25
  39.3 1.2 copy-start.3
  40.0 1.8 copy-start.2
  42.8 82.6 %copy-start.5 = (f32[9]{0:T(128)S(1)}, f32[9]{0:T(128)}, u32[]{:S(2)}) copy-start(f32[9]{0:T(128)} %param.11) | copy-start | bytes 112
  216.8 2.0 copy-start.4
